TPU v7x, 128 devices: a whole 4x4x4 slice. The times are simulated.
128 devices in a mesh: row: 2 (over x_lo), col: 64 (over z, y, x_hi, core).
Axes of the slice: x: 4 (x_hi: 2, x_lo: 2; x = x_hi * 2 + x_lo), y: 4, z: 4, core: 2. Of those that a mesh axis runs over, the one named last changes fastest.
Arguments:
- panel: bfloat16 [196608, 1024], P('col', 'row'), may hold values from -0.1875 to 0.1875
- rhs: float32 [1024, 196608], P('row', 'col'), may hold values from -6 to 6
- diag_inverse: bfloat16 [2, 512, 512], replicated, may hold values from -1 to 2, as said below
Outputs:
- solved: bfloat16 [1024, 1024], P(None, 'row')
- updated: float32 [1024, 196608], P('row', 'col')
Inputs may be any that keep to these rules, and one draw needn't show every extreme that they name: `diag_inverse`: each block is lower triangular; its diagonal entries are 0.5 or more.
All inputs are finite; a program needn't handle non-finite values.
Results may differ from a plain program's by a relative error of at most 0.0065.
Values may be sent and summed in bfloat16 or wider, within the bound.
No kernel may reach another device: no remote copies, remote signals or barrier semaphores. Data moves between devices by JAX's collectives and lax.ppermute only.
A program may use at most 128 MiB of HBM per device.

v0:
```python
import jax
import jax.numpy as jnp
from jax import lax
from jax.sharding import PartitionSpec as P


def rows_for(lines, length):
    spare = -len(lines) % length
    return jnp.pad(lines, [(0, spare)] + [(0, 0)] * (lines.ndim - 1))


def broadcast_by_parts(value, axis, root):
    lines = jnp.where(lax.axis_index(axis) == root, value, jnp.zeros_like(value)).reshape(
        -1, *value.shape[1:][-1:]
    )
    padded = rows_for(lines, lax.axis_size(axis))
    own = lax.psum_scatter(padded, axis, scatter_dimension=0, tiled=True)
    return lax.all_gather(own, axis, axis=0, tiled=True)[: len(lines)].reshape(value.shape)


def from_everyone(value, axis):
    copies = jnp.broadcast_to(value, (lax.axis_size(axis), *value.shape))
    return lax.all_to_all(copies, axis, split_axis=0, concat_axis=0, tiled=True)


def taken_together(value, axis):
    return from_everyone(value, axis).sum(axis=0)


def split_up(value, dim, length):
    lengths = value.shape
    tiles = value.reshape(*lengths[:dim], length, lengths[dim] // length, *lengths[dim + 1 :])
    return jnp.moveaxis(tiles, dim, 0)


def sum_at_owner(value, axis, dim):
    tiles = split_up(value, dim, lax.axis_size(axis))
    arrived = lax.all_to_all(tiles, axis, split_axis=0, concat_axis=0, tiled=True)
    return arrived.astype(jnp.float32).sum(axis=0)


def spread_block(values, owner):
    return broadcast_by_parts(values, "col", owner)


def shards(panel, rhs, diag_inverse):
    block_size = diag_inverse.shape[1]
    step_count = diag_inverse.shape[0]
    rows_dev = panel.shape[0]
    slice_count = rhs.shape[0]
    rhs_count = slice_count * lax.axis_size("row")
    row_index = lax.axis_index("row")
    col_index = lax.axis_index("col")
    dropped = (col_index < step_count) & (row_index >= col_index)
    top_block = jnp.where(dropped, jnp.zeros_like(panel[:block_size]), panel[:block_size])
    masked = jnp.concatenate([top_block, panel[block_size:]], axis=0)
    contract = (((1,), (1,)), ((), ()))
    own_solved = jnp.zeros((rhs_count, block_size), jnp.bfloat16)
    products = jnp.zeros((rhs_count, rows_dev), jnp.float32)
    for current in range(step_count):
        inverse = diag_inverse[current].astype(jnp.float32)
        partial_value = lax.cond(
            col_index == current,
            lambda: lax.dot_general(
                own_solved, masked[:block_size], contract, preferred_element_type=jnp.float32
            ),
            lambda: jnp.zeros((rhs_count, block_size), jnp.float32),
        )
        embedded = lax.dynamic_update_slice(
            jnp.zeros((rhs_count, block_size), jnp.float32),
            rhs[:, :block_size],
            (row_index * slice_count, jnp.int32(0)),
        )
        residual = taken_together(embedded - partial_value, "row")
        whole_block = jnp.dot(residual, inverse.T, precision=lax.Precision.HIGHEST).astype(
            jnp.bfloat16
        )
        arrived = spread_block(whole_block, current)
        own_solved = jnp.where(row_index == current, arrived, own_solved)
        products = lax.cond(
            row_index == current,
            lambda: lax.dot_general(arrived, masked, contract, preferred_element_type=jnp.float32),
            lambda: products,
        )
    reduced = sum_at_owner(products.astype(jnp.bfloat16), "row", 0)
    updated = rhs - reduced
    return (own_solved, updated)


def solution(mesh):
    placed = (P("col", "row"), P("row", "col"), P())
    return jax.shard_map(
        shards,
        mesh=mesh,
        in_specs=placed,
        out_specs=(P(None, "row"), P("row", "col")),
        check_vma=False,
    )
```

profile of v0, /device:TPU:1, one launch (start us, length us, event | category | flops | bytes accessed | tf_op | source)
XLA Modules:
  0.0 1041.3 jit_solution(9920857579655382945)
XLA Ops:
  7.2 0.0 reduce-scatter.3.cloned.1.call-start
  7.2 1.1 slice_select_fusion
  8.3 0.2 broadcast.15
  8.6 1.3 slice_dynamic-update-slice_fusion
  9.9 1.6 conditional.4
  9.9 1.6 broadcast.10
  11.5 2.1 sub.9
  13.5 0.6 broadcast_in_dim.13
  14.1 50.4 %all_to_all.15 = f32[2,1024,512]{2,1,0:T(8,128)} all-to-all(f32[2,1024,512]{2,1,0:T(8,128)S(1)} %broadcast_in_dim.13), channel_id=1, replica_groups=mesh['row'=2,'col'=64] {'row'}, dimensions={0} | all-to-all | bytes 8388608 | tf_op jit(solution)/shard_map/all_to_all | solution.py:23
  64.6 4.2 reduce_sum.27
  68.7 4.5 fusion.3
  73.2 0.0 reduce-scatter.3.cloned.1.call-update
  73.2 0.0 all-gather.3.cloned.1.call-start
  73.3 334.0 %reduce-scatter.3.cloned.1.call-done = bf16[16,512]{1,0:T(8,128)(2,1)} async-done(((bf16[1024,512]{1,0:T(8,128)(2,1)}), bf16[16,512]{1,0:T(8,128)(2,1)}) %reduce-scatter.3.cloned.1.call-update) | async-done | bytes 16400 | tf_op jit(solution)/shard_map/reduce_scatter | solution.py:17
  407.3 0.0 all-gather.3.cloned.1.call-update
  407.3 0.0 reduce-scatter.5.cloned.1.call-start
  407.4 70.8 %all-gather.3.cloned.1.call-done = bf16[1024,512]{1,0:T(8,128)(2,1)} async-done(((bf16[16,512]{1,0:T(8,128)(2,1)}), bf16[1024,512]{1,0:T(8,128)(2,1)}) %all-gather.3.cloned.1.call-update) | async-done | bytes 1048592 | tf_op jit(solution)/shard_map/all_gather | solution.py:18
  478.1 2.3 broadcast_select_fusion
  480.4 3.3 conditional.5
  480.4 3.3 fusion.9
  483.7 2.1 sub.10
  485.8 0.6 broadcast_in_dim.14
  486.4 50.4 %all_to_all.16 = f32[2,1024,512]{2,1,0:T(8,128)} all-to-all(f32[2,1024,512]{2,1,0:T(8,128)S(1)} %broadcast_in_dim.14), channel_id=1, replica_groups=mesh['row'=2,'col'=64] {'row'}, dimensions={0} | all-to-all | bytes 8388608 | tf_op jit(solution)/shard_map/all_to_all | solution.py:23
  536.7 2.9 reduce_sum.28
  539.6 3.9 fusion.4
  543.4 0.0 slice-start
  543.4 0.0 reduce-scatter.5.cloned.1.call-update
  543.5 0.0 all-gather.5.cloned.1.call-start
  543.5 325.5 %reduce-scatter.5.cloned.1.call-done = bf16[16,512]{1,0:T(8,128)(2,1)} async-done(((bf16[1024,512]{1,0:T(8,128)(2,1)}), bf16[16,512]{1,0:T(8,128)(2,1)}) %reduce-scatter.5.cloned.1.call-update) | async-done | bytes 16400 | tf_op jit(solution)/shard_map/reduce_scatter | solution.py:17
  869.0 0.0 all-gather.5.cloned.1.call-update
  869.1 0.0 slice-done
  869.1 1.8 pad_maximum_fusion
  870.9 8.4 conditional.6
  870.9 8.4 fusion.10
  879.3 60.2 %all-gather.5.cloned.1.call-done = bf16[1024,512]{1,0:T(8,128)(2,1)} async-done(((bf16[16,512]{1,0:T(8,128)(2,1)}), bf16[1024,512]{1,0:T(8,128)(2,1)}) %all-gather.5.cloned.1.call-update) | async-done | bytes 1048592 | tf_op jit(solution)/shard_map/all_gather | solution.py:18
  939.5 0.0 copy-start
  939.5 0.0 copy-start.1
  939.5 10.1 all-to-all-start.2
  949.6 0.0 copy-done
  949.6 0.0 copy-done.1
  949.6 1.1 broadcast_select_fusion.1
  950.7 72.5 %all-to-all-done.2 = bf16[2,512,3072]{2,1,0:T(8,128)(2,1)} async-done(((bf16[2,512,3072]{2,1,0:T(8,128)(2,1)}), bf16[2,512,3072]{2,1,0:T(8,128)(2,1)}, u32[]{:S(2)}, u32[]{:S(2)}) %all-to-all-start.2) | async-done | bytes 6291488 | tf_op jit(solution)/shard_map/all_to_all | solution.py:38
  1023.1 5.0 convert_reduce_fusion
  1028.1 6.6 sub.11
  (1 shorter events, 0.0 us)
Async XLA Ops:
  7.2 400.1 %reduce-scatter.3.cloned.1.call-start = ((), (), s32[]{:S(2)}) async-start(), calls=%async_computation.5 | async-start | bytes 1064960 | tf_op jit(solution)/shard_map/reduce_scatter | solution.py:17
  73.2 404.9 %all-gather.3.cloned.1.call-start = ((), (), s32[]{:S(2)}) async-start(), calls=%async_computation.6 | async-start | bytes 1064960 | tf_op jit(solution)/shard_map/all_gather | solution.py:18
  407.3 461.7 %reduce-scatter.5.cloned.1.call-start = ((), (), s32[]{:S(2)}) async-start(), calls=%async_computation.7 | async-start | bytes 1064960 | tf_op jit(solution)/shard_map/reduce_scatter | solution.py:17
  543.4 325.6 %slice-start = ((bf16[3072,512]{1,0:T(8,128)(2,1)}), bf16[2560,512]{1,0:T(8,128)(2,1)S(1)}, s32[]{:S(2)}) async-start(bf16[3072,512]{1,0:T(8,128)(2,1)} %param.11), calls=%async_computation.9 | async-start | bytes 5242880 | tf_op jit(solution)/shard_map/slice | solution.py:56
  543.5 396.0 %all-gather.5.cloned.1.call-start = ((), (), s32[]{:S(2)}) async-start(), calls=%async_computation.8 | async-start | bytes 1064960 | tf_op jit(solution)/shard_map/all_gather | solution.py:18
  939.5 10.1 copy-start
  939.5 10.1 copy-start.1
  939.5 83.6 %all-to-all-start.2 = ((bf16[2,512,3072]{2,1,0:T(8,128)(2,1)}), bf16[2,512,3072]{2,1,0:T(8,128)(2,1)}, u32[]{:S(2)}, u32[]{:S(2)}) async-start(bf16[2,512,3072]{2,1,0:T(8,128)(2,1)} %bitcast.16), calls=%async_computation.4 | async-start | bytes 12582912 | tf_op jit(solution)/shard_map/all_to_all | solution.py:38
Sparse Core Ops, SparseCore 0:
  73.3 333.9 reduce-scatter.2
  410.5 67.5 all-gather.2
  543.6 325.4 reduce-scatter.4
  872.1 67.3 all-gather.4
where the time goes:
time: 1040 us
  waiting for transfers between devices  863 us (83%)
  blocking collectives  101 us (10%)
  other arithmetic  29 us (3%)
  matrix products  20 us (2%)
  between operations  13.8 us (1%)
    reduce_scatter x2, waiting for transfers between devices, broadcast_by_parts(): own = lax.psum_scatter(padded, axis, scatter_dimension=0, tiled=True)  660 us
    all_gather x2, waiting for transfers between devices, broadcast_by_parts(): lax.all_gather(own, axis, axis=0, tiled=True)[:len(lines)]  131 us
    all_to_all x2, blocking collectives, from_everyone(): return lax.all_to_all(copies, axis, split_axis=0, concat_axis=0, tiled=True)  101 us
    all_to_all x1, waiting for transfers between devices, sum_at_owner(): lax.all_to_all(tiles, axis, split_axis=0, concat_axis=0, tiled=True)  72.5 us
  transfers between devices with their start and end apart: 5, of which 5 were waited for; matrix products, arithmetic and copies ran while one was open for 1% of the time, Pallas kernels for 0%

commit v1 on v0

--- a/solution.py
+++ b/solution.py
@@ -15,7 +15,9 @@
     )
     padded = rows_for(lines, lax.axis_size(axis))
     own = lax.psum_scatter(padded, axis, scatter_dimension=0, tiled=True)
-    return lax.all_gather(own, axis, axis=0, tiled=True)[: len(lines)].reshape(value.shape)
+    return jnp.concatenate(
+        lax.all_to_all(jnp.stack([own] * lax.axis_size(axis)), axis, 0, 0), axis=0
+    )[: len(lines)].reshape(value.shape)
 
 
 def from_everyone(value, axis):

time: 1040 us -> 967 us (0.930)
  waiting for transfers between devices: 863 us -> 757 us
  starting transfers between devices: 10.2 us -> 35.1 us
    all_gather x2 -> x0, waiting for transfers between devices: 131 us -> none  [broadcast_by_parts(): lax.all_gather(own, axis, axis=0, tiled=True)[:len(lines)]]
    all_to_all x0 -> x2, waiting for transfers between devices: none -> 27.6 us  [broadcast_by_parts(): lax.all_to_all(jnp.stack([own] * lax.axis_size(axis)), axis, 0, 0)]
    all_to_all x0 -> x2, starting transfers between devices: none -> 24.9 us  [broadcast_by_parts(): lax.all_to_all(jnp.stack([own] * lax.axis_size(axis)), axis, 0, 0)]
where the time goes in v1:
time: 967 us; the launch traced here: 966 us
  waiting for transfers between devices  757 us (78%)
  blocking collectives  101 us (10%)
  starting transfers between devices  35.1 us (4%)
  other arithmetic  29.3 us (3%)
  matrix products  19 us (2%)
  between operations  14.2 us (1%)
  local copies, waits for them, and re-layouts  9.94 us (1%)
    reduce_scatter x2, waiting for transfers between devices, broadcast_by_parts(): own = lax.psum_scatter(padded, axis, scatter_dimension=0, tiled=True)  659 us
    all_to_all x2, blocking collectives, from_everyone(): return lax.all_to_all(copies, axis, split_axis=0, concat_axis=0, tiled=True)  101 us
    all_to_all x1, waiting for transfers between devices, sum_at_owner(): lax.all_to_all(tiles, axis, split_axis=0, concat_axis=0, tiled=True)  71 us
    all_to_all x2, waiting for transfers between devices, broadcast_by_parts(): lax.all_to_all(jnp.stack([own] * lax.axis_size(axis)), axis, 0, 0)  27.6 us
    all_to_all x2, starting transfers between devices, broadcast_by_parts(): lax.all_to_all(jnp.stack([own] * lax.axis_size(axis)), axis, 0, 0)  24.9 us
  transfers between devices with their start and end apart: 5, of which 5 were waited for; matrix products, arithmetic and copies ran while one was open for 1% of the time, Pallas kernels for 0%

profile of v1, /device:TPU:1, one launch (start us, length us, event | category | flops | bytes accessed | tf_op | source)
XLA Modules:
  0.0 965.8 jit_solution(3629831655837502180)
XLA Ops:
  7.2 0.0 reduce-scatter.3.cloned.1.call-start
  7.2 1.1 slice_select_fusion
  8.3 0.0 copy-start.2
  8.3 0.2 broadcast.19
  8.6 1.3 slice_dynamic-update-slice_fusion
  9.9 0.0 copy-done.2
  9.9 1.6 conditional.4
  9.9 1.6 broadcast.14
  11.5 2.1 sub.9
  13.6 0.6 broadcast_in_dim.13
  14.2 50.4 %all_to_all.25 = f32[2,1024,512]{2,1,0:T(8,128)} all-to-all(f32[2,1024,512]{2,1,0:T(8,128)S(1)} %broadcast_in_dim.13), channel_id=1, replica_groups=mesh['row'=2,'col'=64] {'row'}, dimensions={0} | all-to-all | bytes 8388608 | tf_op jit(solution)/shard_map/all_to_all | solution.py:25
  64.6 4.2 reduce_sum.27
  68.8 0.0 copy-done.4
  68.8 4.4 fusion.3
  73.2 0.0 reduce-scatter.3.cloned.1.call-update
  73.2 334.2 %reduce-scatter.3.cloned.1.call-done = bf16[16,512]{1,0:T(8,128)(2,1)} async-done(((bf16[1024,512]{1,0:T(8,128)(2,1)}), bf16[16,512]{1,0:T(8,128)(2,1)}) %reduce-scatter.3.cloned.1.call-update) | async-done | bytes 16400 | tf_op jit(solution)/shard_map/reduce_scatter | solution.py:17
  407.5 1.8 stack.4
  409.3 12.1 %all-to-all-start.1 = ((bf16[64,16,512]{2,1,0:T(8,128)(2,1)}), bf16[64,16,512]{2,1,0:T(8,128)(2,1)S(1)}, u32[]{:S(2)}, u32[]{:S(2)}) async-start(bf16[64,16,512]{2,1,0:T(8,128)(2,1)} %stack.4), calls=%async_computation.2 | async-start | bytes 2097152 | tf_op jit(solution)/shard_map/all_to_all | solution.py:19
  421.4 0.0 reduce-scatter.5.cloned.1.call-start
  421.4 19.9 %all-to-all-done.1 = bf16[64,16,512]{2,1,0:T(8,128)(2,1)S(1)} async-done(((bf16[64,16,512]{2,1,0:T(8,128)(2,1)}), bf16[64,16,512]{2,1,0:T(8,128)(2,1)S(1)}, u32[]{:S(2)}, u32[]{:S(2)}) %all-to-all-start.1) | async-done | bytes 1048608 | tf_op jit(solution)/shard_map/all_to_all | solution.py:19
  441.3 1.2 broadcast_select_fusion
  442.5 0.2 copy-done
  442.7 3.4 conditional.5
  442.7 3.4 fusion.9
  446.1 2.1 sub.10
  448.2 0.6 broadcast_in_dim.14
  448.8 50.5 %all_to_all.26 = f32[2,1024,512]{2,1,0:T(8,128)} all-to-all(f32[2,1024,512]{2,1,0:T(8,128)S(1)} %broadcast_in_dim.14), channel_id=1, replica_groups=mesh['row'=2,'col'=64] {'row'}, dimensions={0} | all-to-all | bytes 8388608 | tf_op jit(solution)/shard_map/all_to_all | solution.py:25
  499.3 2.9 reduce_sum.28
  502.2 0.0 copy-done.5
  502.2 2.8 fusion.4
  505.0 0.0 reduce-scatter.5.cloned.1.call-update
  505.0 324.5 %reduce-scatter.5.cloned.1.call-done = bf16[16,512]{1,0:T(8,128)(2,1)} async-done(((bf16[1024,512]{1,0:T(8,128)(2,1)}), bf16[16,512]{1,0:T(8,128)(2,1)}) %reduce-scatter.5.cloned.1.call-update) | async-done | bytes 16400 | tf_op jit(solution)/shard_map/reduce_scatter | solution.py:17
  829.5 1.8 stack.5
  831.3 12.8 %all-to-all-start.3 = ((bf16[64,16,512]{2,1,0:T(8,128)(2,1)}), bf16[64,16,512]{2,1,0:T(8,128)(2,1)}, u32[]{:S(2)}, u32[]{:S(2)}) async-start(bf16[64,16,512]{2,1,0:T(8,128)(2,1)} %stack.5), calls=%async_computation.5 | async-start | bytes 2097152 | tf_op jit(solution)/shard_map/all_to_all | solution.py:19
  844.2 0.0 slice-start
  844.2 0.0 copy-start.3
  844.2 1.7 slice-done
  845.9 0.1 copy-done.3
  846.0 1.8 pad_maximum_fusion
  847.8 8.4 conditional.6
  847.8 8.4 fusion.10
  856.2 7.8 all-to-all-done.3
  864.0 10.1 %all-to-all-start.4 = ((bf16[2,512,3072]{2,1,0:T(8,128)(2,1)}), bf16[2,512,3072]{2,1,0:T(8,128)(2,1)}, u32[]{:S(2)}, u32[]{:S(2)}) async-start(bf16[2,512,3072]{2,1,0:T(8,128)(2,1)} %bitcast.22), calls=%async_computation.6 | async-start | bytes 12582912 | tf_op jit(solution)/shard_map/all_to_all | solution.py:40
  874.1 0.0 copy-done.1
  874.1 2.3 broadcast_select_fusion.1
  876.4 71.0 %all-to-all-done.4 = bf16[2,512,3072]{2,1,0:T(8,128)(2,1)} async-done(((bf16[2,512,3072]{2,1,0:T(8,128)(2,1)}), bf16[2,512,3072]{2,1,0:T(8,128)(2,1)}, u32[]{:S(2)}, u32[]{:S(2)}) %all-to-all-start.4) | async-done | bytes 6291488 | tf_op jit(solution)/shard_map/all_to_all | solution.py:40
  947.4 5.0 convert_reduce_fusion
  952.4 6.6 sub.11
  (5 shorter events, 0.0 us)
Async XLA Ops:
  7.2 400.3 %reduce-scatter.3.cloned.1.call-start = ((), (), s32[]{:S(2)}) async-start(), calls=%async_computation.7 | async-start | bytes 1064960 | tf_op jit(solution)/shard_map/reduce_scatter | solution.py:17
  8.3 1.6 copy-start.2
  64.6 4.2 copy-start.4
  409.3 32.0 %all-to-all-start.1 = ((bf16[64,16,512]{2,1,0:T(8,128)(2,1)}), bf16[64,16,512]{2,1,0:T(8,128)(2,1)S(1)}, u32[]{:S(2)}, u32[]{:S(2)}) async-start(bf16[64,16,512]{2,1,0:T(8,128)(2,1)} %stack.4), calls=%async_computation.2 | async-start | bytes 2097152 | tf_op jit(solution)/shard_map/all_to_all | solution.py:19
  421.4 408.1 %reduce-scatter.5.cloned.1.call-start = ((), (), s32[]{:S(2)}) async-start(), calls=%async_computation.8 | async-start | bytes 1064960 | tf_op jit(solution)/shard_map/reduce_scatter | solution.py:17
  441.3 1.4 copy-start
  499.3 2.9 copy-start.5
  831.3 32.7 %all-to-all-start.3 = ((bf16[64,16,512]{2,1,0:T(8,128)(2,1)}), bf16[64,16,512]{2,1,0:T(8,128)(2,1)}, u32[]{:S(2)}, u32[]{:S(2)}) async-start(bf16[64,16,512]{2,1,0:T(8,128)(2,1)} %stack.5), calls=%async_computation.5 | async-start | bytes 2097152 | tf_op jit(solution)/shard_map/all_to_all | solution.py:19
  844.2 1.7 slice-start
  844.2 1.8 copy-start.3
  864.0 10.1 %copy-start.1 = (bf16[64,16,512]{2,1,0:T(8,128)(2,1)S(1)}, bf16[64,16,512]{2,1,0:T(8,128)(2,1)}, u32[]{:S(2)}) copy-start(bf16[64,16,512]{2,1,0:T(8,128)(2,1)} %copy-done) | copy-start | bytes 3145732
  864.0 83.4 %all-to-all-start.4 = ((bf16[2,512,3072]{2,1,0:T(8,128)(2,1)}), bf16[2,512,3072]{2,1,0:T(8,128)(2,1)}, u32[]{:S(2)}, u32[]{:S(2)}) async-start(bf16[2,512,3072]{2,1,0:T(8,128)(2,1)} %bitcast.22), calls=%async_computation.6 | async-start | bytes 12582912 | tf_op jit(solution)/shard_map/all_to_all | solution.py:40
Sparse Core Ops, SparseCore 0:
  73.3 334.0 reduce-scatter.2
  505.1 324.3 reduce-scatter.4
